TPU v7x, 32 devices: a whole 2x2x4 slice. The times are simulated.
32 devices in a mesh: ctx: 16 (over z, x, core), shard: 2 (over y).
Axes of the slice: x: 2, y: 2, z: 4, core: 2. Of those that a mesh axis runs over, the one named last changes fastest.
Arguments:
- layer_input: bfloat16 [4096, 1536], P(('ctx', 'shard')), may hold values from -16 to 16
- positions: int32 [4096], replicated, may hold values from 0 to 4095, as said below
- norm_gain_attn: float32 [1536], replicated, may hold values from 0.1 to 1.9
- w_query: bfloat16 [1536, 1536], P('shard'), may hold values from -1 to 1
- key_weight: bfloat16 [1536, 768], P('shard'), may hold values from -1 to 1
- value_weight: bfloat16 [1536, 768], P('shard'), may hold values from -0.15625 to 0.15625
- w_out: bfloat16 [1536, 1536], P('shard'), may hold values from -3.5 to 3.5
- norm_gain_ffn: float32 [1536], replicated, may hold values from 0.1 to 1.9
- w_gate: bfloat16 [1536, 4096], P('shard'), may hold values from -0.15625 to 0.15625
- w_up: bfloat16 [1536, 4096], P('shard'), may hold values from -0.15625 to 0.15625
- w_down: bfloat16 [4096, 1536], P('shard'), may hold values from -0.09375 to 0.09375
- out_cotangent: bfloat16 [4096, 1536], P(('ctx', 'shard')), may hold values from -6 to 6
Outputs:
- layer_output: bfloat16 [4096, 1536], P(('ctx', 'shard'))
- input_grad: bfloat16 [4096, 1536], P(('ctx', 'shard'))
- grad_norm_attn: float32 [1536], P(('ctx', 'shard'))
- grad_query: float32 [1536, 1536], P(('ctx', 'shard'))
- grad_key: float32 [1536, 768], P(('ctx', 'shard'))
- grad_value: float32 [1536, 768], P(('ctx', 'shard'))
- grad_out: float32 [1536, 1536], P(('ctx', 'shard'))
- grad_norm_ffn: float32 [1536], P(('ctx', 'shard'))
- grad_gate: float32 [1536, 4096], P(('ctx', 'shard'))
- grad_up: float32 [1536, 4096], P(('ctx', 'shard'))
- grad_down: float32 [4096, 1536], P(('ctx', 'shard'))
Inputs may be any that keep to these rules, and one draw needn't show every extreme that they name: `positions`: every position 0 to 4095 appears once. The sequence is cut into 2 * 16 blocks of 128 / 2 * 2 rows; a permutation drawn per problem gives each ctx index c a pair number k, and the device of ctx index c and shard index s holds in its first 64 rows the s-th part of block k and in the rest the s-th part of block 2 * 16 - 1 - k, each part in increasing order.
All inputs are finite; a program needn't handle non-finite values.
Results may differ from a plain program's by a relative error of at most 0.025.
Values may be sent and summed in bfloat16 or wider, within the bound.
A program may use at most 512 MiB of HBM per device.

v0:
```python
import math

import jax
import jax.numpy as jnp
from jax import lax
from jax.sharding import PartitionSpec as P

QUERY_HEADS = 16
SHARED_KV_UNITS = 8
CHANNEL_SPAN = 96


epsilon = 1e-05
rope_base = 100000.0
mask_fill_value = -1e30


def rope_tables(positions, head_size):
    half_size = head_size // 2
    frequency = rope_base ** (-2.0 * jnp.arange(half_size, dtype=jnp.float32) / head_size)
    angles = positions.astype(jnp.float32)[:, None] * frequency[None, :]
    return (jnp.cos(angles)[:, None, :], jnp.sin(angles)[:, None, :])


def apply_rotary(value_matrix, cosine_table, sine_table):
    half_size = value_matrix.shape[-1] // 2
    first_half = value_matrix[..., :half_size]
    second_half = value_matrix[..., half_size:]
    return jnp.concatenate(
        [
            first_half * cosine_table - second_half * sine_table,
            second_half * cosine_table + first_half * sine_table,
        ],
        axis=-1,
    )


def back_project(gradient, weight):
    return lax.dot_general(
        gradient, weight, (((1,), (1,)), ((), ())), preferred_element_type=jnp.float32
    )


def weight_grad(inputs, gradient):
    return lax.dot_general(
        inputs, gradient, (((0,), (0,)), ((), ())), preferred_element_type=jnp.float32
    )


def rms_backward(grad_normed, normed, inverse_rms, gain):
    scaled = grad_normed * gain
    inner = jnp.mean(scaled * normed, axis=-1, keepdims=True)
    return (inverse_rms * (scaled - normed * inner), jnp.sum(grad_normed * normed, axis=0))


def score_block(query_part, key_block, query_pos, key_pos, scale):
    scores = (
        jnp.einsum("tgjd,sgd->gjts", query_part, key_block, preferred_element_type=jnp.float32)
        * scale
    )
    allowed = key_pos[None, :] <= query_pos[:, None]
    return jnp.where(allowed[None, None], scores, mask_fill_value)


def query_grads(
    query_part,
    grad_part,
    log_part,
    delta_part,
    query_pos,
    key_block_list,
    value_block_list,
    key_positions,
    scale,
):

    def grad_step(query_sum, item):
        key_block, value_block, key_pos = item
        weights = jnp.exp(
            score_block(query_part, key_block, query_pos, key_pos, scale) - log_part[..., None]
        )
        grad_weights = jnp.einsum(
            "tgjd,sgd->gjts", grad_part, value_block, preferred_element_type=jnp.float32
        )
        grad_scores = (weights * (grad_weights - delta_part[..., None])).astype(jnp.bfloat16)
        query_sum = (
            query_sum
            + jnp.einsum(
                "gjts,sgd->tgjd", grad_scores, key_block, preferred_element_type=jnp.float32
            )
            * scale
        )
        return (query_sum, None)

    start = jnp.zeros(query_part.shape, jnp.float32)
    query_sum, unused = lax.scan(
        grad_step, start, (key_block_list, value_block_list, key_positions)
    )
    return query_sum


def key_side_fold(own_keys, own_values, own_pos, all_positions, groups, head_group, scale):

    def fold(carry, piece, start):
        query_piece, grad_piece, log_piece, delta_piece = piece
        rows = query_piece.shape[0]
        block = math.gcd(rows, 512)
        count = rows // block

        def inner(totals, index):
            first = index * block
            query_block = (
                lax.dynamic_slice_in_dim(query_piece, first, block)
                .astype(jnp.bfloat16)
                .reshape(block, groups, head_group, CHANNEL_SPAN)
            )
            grad_block = (
                lax.dynamic_slice_in_dim(grad_piece, first, block)
                .astype(jnp.bfloat16)
                .reshape(block, groups, head_group, CHANNEL_SPAN)
            )
            log_block = jnp.transpose(
                lax.dynamic_slice_in_dim(log_piece, first, block).reshape(
                    block, groups, head_group
                ),
                (1, 2, 0),
            )
            delta_block = jnp.transpose(
                lax.dynamic_slice_in_dim(delta_piece, first, block).reshape(
                    block, groups, head_group
                ),
                (1, 2, 0),
            )
            query_pos = lax.dynamic_slice_in_dim(all_positions, first, block)
            weights = jnp.exp(
                score_block(query_block, own_keys, query_pos, own_pos, scale) - log_block[..., None]
            )
            value_part = jnp.einsum(
                "gjts,tgjd->sgd",
                weights.astype(jnp.bfloat16),
                grad_block,
                preferred_element_type=jnp.float32,
            )
            grad_weights = jnp.einsum(
                "tgjd,sgd->gjts", grad_block, own_values, preferred_element_type=jnp.float32
            )
            grad_scores = (weights * (grad_weights - delta_block[..., None])).astype(jnp.bfloat16)
            key_part = (
                jnp.einsum(
                    "gjts,tgjd->sgd", grad_scores, query_block, preferred_element_type=jnp.float32
                )
                * scale
            )
            return ((totals[0] + key_part, totals[1] + value_part), None)

        carry, unused = lax.scan(inner, carry, jnp.arange(count, dtype=jnp.int32))
        return carry

    return fold


def body(
    layer_input,
    positions,
    norm_gain_attn,
    w_query,
    key_weight,
    value_weight,
    w_out,
    norm_gain_ffn,
    w_gate,
    w_up,
    w_down,
    out_cotangent,
):
    row_total = layer_input.shape[0]
    head_group = QUERY_HEADS // SHARED_KV_UNITS
    scale = 1.0 / math.sqrt(CHANNEL_SPAN)
    overall_accumulator = positions.shape[0]
    key_row_values = math.gcd(overall_accumulator, 1024)
    key_total_count = overall_accumulator // key_row_values
    first_row = lax.axis_index(("ctx", "shard")) * row_total
    own_positions = lax.dynamic_slice_in_dim(positions, first_row, row_total)
    cosine_table, sine_table = rope_tables(own_positions, CHANNEL_SPAN)
    wq_full, wk_full, wv_full, wo_full = (
        lax.all_gather(w_query, "shard", axis=0, tiled=True),
        lax.all_gather(key_weight, "shard", axis=0, tiled=True),
        lax.all_gather(value_weight, "shard", axis=0, tiled=True),
        lax.all_gather(w_out, "shard", axis=0, tiled=True),
    )
    resid_in = layer_input.astype(jnp.float32)
    inverse_one = lax.rsqrt(jnp.mean(resid_in * resid_in, axis=-1, keepdims=True) + epsilon)
    normed_one = resid_in * inverse_one
    attention_normed = (normed_one * norm_gain_attn).astype(jnp.bfloat16)
    query_matrix = apply_rotary(
        jnp.dot(attention_normed, wq_full, preferred_element_type=jnp.float32).reshape(
            row_total, QUERY_HEADS, CHANNEL_SPAN
        ),
        cosine_table,
        sine_table,
    ).astype(jnp.bfloat16)
    keys_local = (
        apply_rotary(
            jnp.dot(attention_normed, wk_full, preferred_element_type=jnp.float32).reshape(
                row_total, SHARED_KV_UNITS, CHANNEL_SPAN
            ),
            cosine_table,
            sine_table,
        )
        .astype(jnp.bfloat16)
        .reshape(row_total, SHARED_KV_UNITS * CHANNEL_SPAN)
    )
    values_local = jnp.dot(attention_normed, wv_full, preferred_element_type=jnp.float32).astype(
        jnp.bfloat16
    )
    grouped_queries = query_matrix.reshape(row_total, SHARED_KV_UNITS, head_group, CHANNEL_SPAN)
    key_positions = positions.reshape(key_total_count, key_row_values)
    every_key, every_value = (
        lax.all_gather(keys_local, ("ctx", "shard"), axis=0, tiled=True),
        lax.all_gather(values_local, ("ctx", "shard"), axis=0, tiled=True),
    )
    key_block_list = every_key.reshape(
        key_total_count, key_row_values, SHARED_KV_UNITS, CHANNEL_SPAN
    )
    value_block_list = every_value.reshape(
        key_total_count, key_row_values, SHARED_KV_UNITS, CHANNEL_SPAN
    )

    def total_step(carry, item):
        largest, running = carry
        key_block, key_pos = item
        scores = score_block(grouped_queries, key_block, own_positions, key_pos, scale)
        new_largest = jnp.maximum(largest, jnp.max(scores, axis=-1))
        running = running * jnp.exp(largest - new_largest) + jnp.sum(
            jnp.exp(scores - new_largest[..., None]), axis=-1
        )
        return ((new_largest, running), None)

    initial_largest = jnp.full(
        (SHARED_KV_UNITS, head_group, row_total), mask_fill_value, jnp.float32
    )
    (largest, running), unused = lax.scan(
        total_step,
        (initial_largest, jnp.zeros((SHARED_KV_UNITS, head_group, row_total), jnp.float32)),
        (key_block_list, key_positions),
    )
    log_total = largest + jnp.log(running)

    def mix_step(mixed, item):
        key_block, value_block, key_pos = item
        weights = jnp.exp(
            score_block(grouped_queries, key_block, own_positions, key_pos, scale)
            - log_total[..., None]
        ).astype(jnp.bfloat16)
        return (
            mixed
            + jnp.einsum(
                "gjts,sgd->tgjd", weights, value_block, preferred_element_type=jnp.float32
            ),
            None,
        )

    mixed, unused = lax.scan(
        mix_step,
        jnp.zeros((row_total, SHARED_KV_UNITS, head_group, CHANNEL_SPAN), jnp.float32),
        (key_block_list, value_block_list, key_positions),
    )
    attention_output = mixed.reshape(row_total, QUERY_HEADS * CHANNEL_SPAN).astype(jnp.bfloat16)
    resid_mid = resid_in + jnp.dot(attention_output, wo_full, preferred_element_type=jnp.float32)
    inverse_two = lax.rsqrt(jnp.mean(resid_mid * resid_mid, axis=-1, keepdims=True) + epsilon)
    normed_two = resid_mid * inverse_two
    normed_ffn = (normed_two * norm_gain_ffn).astype(jnp.bfloat16)
    wg_full, wu_full, wd_full = (
        lax.all_gather(w_gate, "shard", axis=0, tiled=True),
        lax.all_gather(w_up, "shard", axis=0, tiled=True),
        lax.all_gather(w_down, "shard", axis=0, tiled=True),
    )
    gate = jnp.dot(normed_ffn, wg_full, preferred_element_type=jnp.float32)
    upward = jnp.dot(normed_ffn, wu_full, preferred_element_type=jnp.float32)
    sigmoid = jax.nn.sigmoid(gate)
    swish = gate * sigmoid
    hidden = (swish * upward).astype(jnp.bfloat16)
    layer_output = (
        resid_mid + jnp.dot(hidden, wd_full, preferred_element_type=jnp.float32)
    ).astype(jnp.bfloat16)
    local_down = weight_grad(hidden, out_cotangent)
    grad_hidden = back_project(out_cotangent, wd_full)
    grad_gate_act = (grad_hidden * upward * sigmoid * (1.0 + gate * (1.0 - sigmoid))).astype(
        jnp.bfloat16
    )
    grad_up_act = (grad_hidden * swish).astype(jnp.bfloat16)
    local_gate = weight_grad(normed_ffn, grad_gate_act)
    local_up = weight_grad(normed_ffn, grad_up_act)
    grad_normed_two = back_project(grad_gate_act, wg_full) + back_project(grad_up_act, wu_full)
    grad_resid_part, local_gain_ffn = rms_backward(
        grad_normed_two, normed_two, inverse_two, norm_gain_ffn
    )
    grad_gate, grad_up, grad_down, grad_norm_ffn = (
        lax.psum_scatter(local_gate, ("ctx", "shard"), scatter_dimension=0, tiled=True),
        lax.psum_scatter(local_up, ("ctx", "shard"), scatter_dimension=0, tiled=True),
        lax.psum_scatter(local_down, ("ctx", "shard"), scatter_dimension=0, tiled=True),
        lax.psum_scatter(local_gain_ffn, ("ctx", "shard"), scatter_dimension=0, tiled=True),
    )
    grad_resid_mid = out_cotangent.astype(jnp.float32) + grad_resid_part
    grad_mid_low = grad_resid_mid.astype(jnp.bfloat16)
    local_out = weight_grad(attention_output, grad_mid_low)
    attention_gradient = back_project(grad_mid_low, wo_full).astype(jnp.bfloat16)
    grouped_gradient = attention_gradient.reshape(
        row_total, SHARED_KV_UNITS, head_group, CHANNEL_SPAN
    )
    delta_row_values = jnp.sum(
        (attention_gradient.astype(jnp.float32) * attention_output.astype(jnp.float32)).reshape(
            row_total, SHARED_KV_UNITS, head_group, CHANNEL_SPAN
        ),
        axis=-1,
    )
    delta_heads = jnp.transpose(delta_row_values, (1, 2, 0))
    log_rows = jnp.transpose(log_total, (2, 0, 1)).reshape(row_total, QUERY_HEADS)
    delta_flat = delta_row_values.reshape(row_total, QUERY_HEADS)
    query_wire = query_matrix.reshape(row_total, QUERY_HEADS * CHANNEL_SPAN).astype(jnp.float32)
    gradient_wire = attention_gradient.astype(jnp.float32)
    query_sum = query_grads(
        grouped_queries,
        grouped_gradient,
        log_total,
        delta_heads,
        own_positions,
        key_block_list,
        value_block_list,
        key_positions,
        scale,
    )
    own_keys = keys_local.reshape(row_total, SHARED_KV_UNITS, CHANNEL_SPAN)
    own_values = values_local.reshape(row_total, SHARED_KV_UNITS, CHANNEL_SPAN)
    folder = key_side_fold(
        own_keys, own_values, own_positions, positions, SHARED_KV_UNITS, head_group, scale
    )
    empty_rows = jnp.zeros((row_total, SHARED_KV_UNITS, CHANNEL_SPAN), jnp.float32)
    owned_keys, value_owned = folder(
        (empty_rows, empty_rows),
        (
            lax.all_gather(query_wire, ("ctx", "shard"), axis=0, tiled=True),
            lax.all_gather(gradient_wire, ("ctx", "shard"), axis=0, tiled=True),
            lax.all_gather(log_rows, ("ctx", "shard"), axis=0, tiled=True),
            lax.all_gather(delta_flat, ("ctx", "shard"), axis=0, tiled=True),
        ),
        jnp.int32(0),
    )
    grad_queries = (
        apply_rotary(
            query_sum.reshape(row_total, QUERY_HEADS, CHANNEL_SPAN), cosine_table, -sine_table
        )
        .astype(jnp.bfloat16)
        .reshape(row_total, QUERY_HEADS * CHANNEL_SPAN)
    )
    key_gradients = (
        apply_rotary(owned_keys, cosine_table, -sine_table)
        .astype(jnp.bfloat16)
        .reshape(row_total, SHARED_KV_UNITS * CHANNEL_SPAN)
    )
    value_gradients = value_owned.astype(jnp.bfloat16).reshape(
        row_total, SHARED_KV_UNITS * CHANNEL_SPAN
    )
    local_query = weight_grad(attention_normed, grad_queries)
    local_key = weight_grad(attention_normed, key_gradients)
    local_value = weight_grad(attention_normed, value_gradients)
    grad_normed_one = (
        back_project(grad_queries, wq_full)
        + back_project(key_gradients, wk_full)
        + back_project(value_gradients, wv_full)
    )
    grad_resid_in, local_gain_attn = rms_backward(
        grad_normed_one, normed_one, inverse_one, norm_gain_attn
    )
    grad_query, grad_key, grad_value, grad_out, grad_norm_attn = (
        lax.psum_scatter(local_query, ("ctx", "shard"), scatter_dimension=0, tiled=True),
        lax.psum_scatter(local_key, ("ctx", "shard"), scatter_dimension=0, tiled=True),
        lax.psum_scatter(local_value, ("ctx", "shard"), scatter_dimension=0, tiled=True),
        lax.psum_scatter(local_out, ("ctx", "shard"), scatter_dimension=0, tiled=True),
        lax.psum_scatter(local_gain_attn, ("ctx", "shard"), scatter_dimension=0, tiled=True),
    )
    input_grad = (grad_resid_mid + grad_resid_in).astype(jnp.bfloat16)
    return (
        layer_output,
        input_grad,
        grad_norm_attn,
        grad_query,
        grad_key,
        grad_value,
        grad_out,
        grad_norm_ffn,
        grad_gate,
        grad_up,
        grad_down,
    )


def solution(mesh):
    placed = (
        P(("ctx", "shard"), None),
        P(),
        P(),
        P("shard", None),
        P("shard", None),
        P("shard", None),
        P("shard", None),
        P(),
        P("shard", None),
        P("shard", None),
        P("shard", None),
        P(("ctx", "shard"), None),
    )
    return jax.shard_map(
        body,
        mesh=mesh,
        in_specs=placed,
        out_specs=(
            P(("ctx", "shard"), None),
            P(("ctx", "shard"), None),
            P(("ctx", "shard")),
            P(("ctx", "shard"), None),
            P(("ctx", "shard"), None),
            P(("ctx", "shard"), None),
            P(("ctx", "shard"), None),
            P(("ctx", "shard")),
            P(("ctx", "shard"), None),
            P(("ctx", "shard"), None),
            P(("ctx", "shard"), None),
        ),
        check_vma=False,
    )
```

profile of v0, /device:TPU:0, one launch (start us, length us, event | category | flops | bytes accessed | tf_op | source)
XLA Modules:
  0.0 2311.9 jit_solution(13386923850757972462)
XLA Ops:
  9.7 38.7 %all-gather.12.cloned.1.call-done = bf16[1536,768]{1,0:T(8,128)(2,1)} async-done(((bf16[768,768]{1,0:T(8,128)(2,1)}), bf16[1536,768]{1,0:T(8,128)(2,1)}) %all-gather.12.cloned.1.call-update) | async-done | bytes 2359312 | tf_op jit(solution)/shard_map/all_gather | solution.py:188
  52.2 33.8 %all-gather.16.cloned.1.call-done = bf16[1536,768]{1,0:T(8,128)(2,1)} async-done(((bf16[768,768]{1,0:T(8,128)(2,1)}), bf16[1536,768]{1,0:T(8,128)(2,1)}) %all-gather.16.cloned.1.call-update) | async-done | bytes 2359312 | tf_op jit(solution)/shard_map/all_gather | solution.py:187
  92.4 57.8 %all-gather.20.cloned.1.call-done = bf16[1536,1536]{1,0:T(8,128)(2,1)} async-done(((bf16[768,1536]{1,0:T(8,128)(2,1)}), bf16[1536,1536]{1,0:T(8,128)(2,1)}) %all-gather.20.cloned.1.call-update) | async-done | bytes 4718608 | tf_op jit(solution)/shard_map/all_gather | solution.py:186
  156.1 66.7 %all-gather.14.cloned.1.call-done = bf16[4096,768]{1,0:T(8,128)(2,1)} async-done(((bf16[128,768]{1,0:T(8,128)(2,1)}), bf16[4096,768]{1,0:T(8,128)(2,1)}) %all-gather.14.cloned.1.call-update) | async-done | bytes 6291472 | tf_op jit(solution)/shard_map/all_gather | solution.py:220
  222.8 14.8 reshape.334
  237.6 11.9 copy.60
  249.5 53.2 %all-gather.18.cloned.1.call-done = bf16[4096,768]{0,1:T(8,128)(2,1)} async-done(((bf16[128,768]{0,1:T(8,128)(2,1)}), bf16[4096,768]{0,1:T(8,128)(2,1)}) %all-gather.18.cloned.1.call-update) | async-done | bytes 6291472 | tf_op jit(solution)/shard_map/all_gather | solution.py:219
  302.8 11.4 reshape.311
  314.2 7.9 copy.61
  322.1 46.2 %while.48 = (s32[]{:T(128)}, f32[8,2,128]{2,1,0:T(2,128)S(1)}, f32[8,2,128]{2,1,0:T(2,128)S(1)}, s32[4,1024]{1,0:T(4,128)S(1)}, s32[128]{0:T(128)S(1)}, /*index=...) while((s32[]{:T(128)}, f32[8,2,128]{2,1,0:T(2,128)S(1)}, ...), condition=%wide.region_4.5_spmd.clone, body=%wide.region_1.4_spmd.clone.sunk | while | flops 417474560 | bytes 19255928 | solution.py:242
  368.3 22.3 while.49
  395.1 124.0 %all-gather.24.cloned.1.call-done = bf16[1536,4096]{1,0:T(8,128)(2,1)} async-done(((bf16[768,4096]{1,0:T(8,128)(2,1)}), bf16[1536,4096]{1,0:T(8,128)(2,1)}) %all-gather.24.cloned.1.call-update) | async-done | bytes 12582928 | tf_op jit(solution)/shard_map/all_gather | solution.py:274
  526.8 146.4 %all-gather.26.cloned.1.call-done = bf16[1536,4096]{1,0:T(8,128)(2,1)} async-done(((bf16[768,4096]{1,0:T(8,128)(2,1)}), bf16[1536,4096]{1,0:T(8,128)(2,1)}) %all-gather.26.cloned.1.call-update) | async-done | bytes 12582928 | tf_op jit(solution)/shard_map/all_gather | solution.py:275
  680.9 146.3 %all-gather.28.cloned.1.call-done = bf16[4096,1536]{1,0:T(8,128)(2,1)} async-done(((bf16[2048,1536]{1,0:T(8,128)(2,1)}), bf16[4096,1536]{1,0:T(8,128)(2,1)}) %all-gather.28.cloned.1.call-update) | async-done | bytes 12582928 | tf_op jit(solution)/shard_map/all_gather | solution.py:276
  827.3 11.8 multiply_convert_fusion
  839.1 10.3 fusion.144
  867.1 61.3 %while.50 = (s32[]{:T(128)}, f32[128,8,2,96]{0,3,2,1:T(8,128)}, bf16[4,1024,8,96]{1,3,2,0:T(8,128)(2,1)}, s32[4,1024]{1,0:T(4,128)S(1)}, s32[128]{0:T(128)S(1)},...) while((s32[]{:T(128)}, f32[128,8,2,96]{0,3,2,1:T(8,128)}, ...), condition=%wide.region_11.12_spmd.clone, body=%wide.region_10.11_spmd.clone.sunk | while | flops 1221263360 | bytes 30439620 | solution.py:96
  873.5 7.9 fusion.234
  888.5 9.0 fusion.234
  904.7 7.8 fusion.234
  936.6 74.8 %all_gather.49 = f32[4096,16]{0,1:T(8,128)} all-gather(f32[128,16]{0,1:T(8,128)S(1)} %bitcast.369), channel_id=1, replica_groups=mesh['ctx'=16,'shard'=2] {'ctx','shard'}, dimensions={0}, use_global_device_ids=true | all-gather | bytes 270336 | tf_op jit(solution)/shard_map/all_gather | solution.py:344
  1011.5 71.8 %all_gather.51 = f32[4096,16]{0,1:T(8,128)} all-gather(f32[128,16]{0,1:T(8,128)S(1)} %bitcast.367), channel_id=1, replica_groups=mesh['ctx'=16,'shard'=2] {'ctx','shard'}, dimensions={0}, use_global_device_ids=true | all-gather | bytes 270336 | tf_op jit(solution)/shard_map/all_gather | solution.py:345
  1088.4 195.0 %while.51 = (s32[]{:T(128)}, f32[128,8,96]{0,2,1:T(8,128)}, f32[128,8,96]{0,2,1:T(8,128)}, s32[8]{0:T(128)S(1)}, bf16[4096,1536]{0,1:T(8,128)(2,1)}, /*index=5*/...) while((s32[]{:T(128)}, f32[128,8,96]{0,2,1:T(8,128)}, ...), condition=%wide.region_13.14_spmd.clone, body=%wide.region_12.13_spmd.clone.sunk | while | flops 816349184 | bytes 37133380 | solution.py:156
  1291.4 10.2 fusion.146
  1302.8 10.3 fusion.147
  1314.4 10.4 fusion.148
  1341.3 37.2 %all-reduce.2 = (f32[1536]{0:T(1024)S(1)}, f32[1536]{0:T(1024)S(1)}) all-reduce(f32[1536]{0:T(1024)} %get-tuple-element.438, f32[1536]{0:T(1024)} %get-tuple-element.436), channel_id=2, replica_groups=mesh['ctx'=16,'shard'=2] {'ctx','shard'}, use_global_device_ids=true, to_apply=%region_16.17.clone | all-reduce | flops 3072 | bytes 24576
  1381.8 62.9 %reduce-scatter.10.cloned.1.call-done = f32[48,768]{1,0:T(8,128)} async-done(((f32[1536,768]{1,0:T(8,128)}), f32[48,768]{1,0:T(8,128)}) %reduce-scatter.10.cloned.1.call-update) | async-done | bytes 147472 | tf_op jit(solution)/shard_map/reduce_scatter | solution.py:377
  1444.7 112.3 %reduce-scatter.12.cloned.1.call-done = f32[48,768]{1,0:T(8,128)} async-done(((f32[1536,768]{1,0:T(8,128)}), f32[48,768]{1,0:T(8,128)}) %reduce-scatter.12.cloned.1.call-update) | async-done | bytes 147472 | tf_op jit(solution)/shard_map/reduce_scatter | solution.py:378
  1557.0 248.9 %reduce-scatter.16.cloned.1.call-done = f32[48,4096]{1,0:T(8,128)} async-done(((f32[1536,4096]{1,0:T(8,128)}), f32[48,4096]{1,0:T(8,128)}) %reduce-scatter.16.cloned.1.call-update) | async-done | bytes 786448 | tf_op jit(solution)/shard_map/reduce_scatter | solution.py:299
  1806.0 249.5 %reduce-scatter.18.cloned.1.call-done = f32[48,4096]{1,0:T(8,128)} async-done(((f32[1536,4096]{1,0:T(8,128)}), f32[48,4096]{1,0:T(8,128)}) %reduce-scatter.18.cloned.1.call-update) | async-done | bytes 786448 | tf_op jit(solution)/shard_map/reduce_scatter | solution.py:300
  2055.4 249.4 %reduce-scatter.20.cloned.1.call-done = f32[128,1536]{1,0:T(8,128)} async-done(((f32[4096,1536]{1,0:T(8,128)}), f32[128,1536]{1,0:T(8,128)}) %reduce-scatter.20.cloned.1.call-update) | async-done | bytes 786448 | tf_op jit(solution)/shard_map/reduce_scatter | solution.py:301
  (370 shorter events, 392.8 us)
Async XLA Ops:
  7.2 41.2 %copy-start.28 = (f32[1536]{0:T(1024)S(1)}, f32[1536]{0:T(1024)}, u32[]{:S(2)}) copy-start(f32[1536]{0:T(1024)} %param.22) | copy-start | bytes 18436
  7.2 44.1 %copy-start.33 = (s32[4096]{0:T(1024)S(1)}, s32[4096]{0:T(1024)}, u32[]{:S(2)}) copy-start(s32[4096]{0:T(1024)} %param.21) | copy-start | bytes 49156
  7.2 41.2 %all-gather.12.cloned.1.call-start = ((), (), s32[]{:S(2)}) async-start(), calls=%async_computation.7 | async-start | bytes 3538944 | tf_op jit(solution)/shard_map/all_gather | solution.py:188
  7.9 78.0 %all-gather.16.cloned.1.call-start = ((), (), s32[]{:S(2)}) async-start(), calls=%async_computation.9 | async-start | bytes 3538944 | tf_op jit(solution)/shard_map/all_gather | solution.py:187
  8.7 141.5 %all-gather.20.cloned.1.call-start = ((), (), s32[]{:S(2)}) async-start(), calls=%async_computation.11 | async-start | bytes 7077888 | tf_op jit(solution)/shard_map/all_gather | solution.py:186
  9.4 213.4 %all-gather.14.cloned.1.call-start = ((), (), s32[]{:S(2)}) async-start(), calls=%async_computation.8 | async-start | bytes 6488064 | tf_op jit(solution)/shard_map/all_gather | solution.py:220
  51.3 251.5 %all-gather.18.cloned.1.call-start = ((), (), s32[]{:S(2)}) async-start(), calls=%async_computation.10 | async-start | bytes 6488064 | tf_op jit(solution)/shard_map/all_gather | solution.py:219
  52.2 876.2 %copy-start.29 = (f32[128,48]{0,1:T(8,128)}, f32[128,48]{0,1:T(8,128)S(1)}, u32[]{:S(2)}) copy-start(f32[128,48]{0,1:T(8,128)S(1)} %get-tuple-element.535) | copy-start | bytes 73732
  89.5 302.1 %all-gather.22.cloned.1.call-start = ((), (), s32[]{:S(2)}) async-start(), calls=%async_computation.12 | async-start | bytes 7077888 | tf_op jit(solution)/shard_map/all_gather | solution.py:189
  90.1 429.0 %all-gather.24.cloned.1.call-start = ((), (), s32[]{:S(2)}) async-start(), calls=%async_computation.13 | async-start | bytes 18874368 | tf_op jit(solution)/shard_map/all_gather | solution.py:274
  90.8 582.3 %all-gather.26.cloned.1.call-start = ((), (), s32[]{:S(2)}) async-start(), calls=%async_computation.14 | async-start | bytes 18874368 | tf_op jit(solution)/shard_map/all_gather | solution.py:275
  91.6 735.7 %all-gather.28.cloned.1.call-start = ((), (), s32[]{:S(2)}) async-start(), calls=%async_computation.15 | async-start | bytes 18874368 | tf_op jit(solution)/shard_map/all_gather | solution.py:276
  92.3 996.0 %all-gather.30.cloned.1.call-start = ((), (), s32[]{:S(2)}) async-start(), calls=%async_computation.16 | async-start | bytes 12976128 | tf_op jit(solution)/shard_map/all_gather | solution.py:342
  155.4 932.9 %all-gather.32.cloned.1.call-start = ((), (), s32[]{:S(2)}) async-start(), calls=%async_computation.17 | async-start | bytes 12976128 | tf_op jit(solution)/shard_map/all_gather | solution.py:343
  394.9 462.0 %copy-start.3 = (f32[128,1536]{1,0:T(8,128)}, f32[128,1536]{1,0:T(8,128)S(1)}, u32[]{:S(2)}) copy-start(f32[128,1536]{1,0:T(8,128)S(1)} %get-tuple-element.537) | copy-start | bytes 2359300
  395.1 278.1 %copy-start.5 = (bf16[128,1536]{1,0:T(8,128)(2,1)}, bf16[128,1536]{1,0:T(8,128)(2,1)S(1)}, u32[]{:S(2)}) copy-start(bf16[128,1536]{1,0:T(8,128)(2,1)S(1)} %multiply_convert_fusion.3) | copy-start | bytes 1179652
  526.8 300.5 %copy-start.24 = (bf16[128,1536]{1,0:T(8,128)(2,1)S(1)}, bf16[128,1536]{1,0:T(8,128)(2,1)}, u32[]{:S(2)}) copy-start(bf16[128,1536]{1,0:T(8,128)(2,1)} %param.31) | copy-start | bytes 1179652
  839.0 10.3 copy-start
  849.4 9.0 copy-start.23
  858.4 224.8 %copy-start.7 = (f32[128,1536]{1,0:T(8,128)}, f32[128,1536]{1,0:T(8,128)S(1)}, u32[]{:S(2)}) copy-start(f32[128,1536]{1,0:T(8,128)S(1)} %multiply_add_fusion) | copy-start | bytes 2359300
  863.5 518.3 %reduce-scatter.8.cloned.1.call-start = ((), (), s32[]{:S(2)}) async-start(), calls=%async_computation.18 | async-start | bytes 9732096 | tf_op jit(solution)/shard_map/reduce_scatter | solution.py:376
  867.1 61.3 %copy-start.31 = (f32[128,48]{0,1:T(8,128)S(1)}, f32[128,48]{0,1:T(8,128)}, u32[]{:S(2)}) copy-start(f32[128,48]{0,1:T(8,128)} %get-tuple-element.533) | copy-start | bytes 73732
  934.9 148.3 %copy-start.12 = (bf16[128,8,2,96]{0,3,2,1:T(8,128)(2,1)S(1)}, bf16[128,8,2,96]{0,3,2,1:T(8,128)(2,1)}, u32[]{:S(2)}) copy-start(bf16[128,8,2,96]{0,3,2,1:T(8,128)(2,1)} %copy-done.11) | copy-start | bytes 1179652
  934.9 446.9 %reduce-scatter.14.cloned.1.call-start = ((), (), s32[]{:S(2)}) async-start(), calls=%async_computation.21 | async-start | bytes 9732096 | tf_op jit(solution)/shard_map/reduce_scatter | solution.py:379
  1088.3 356.4 %reduce-scatter.10.cloned.1.call-start = ((), (), s32[]{:S(2)}) async-start(), calls=%async_computation.19 | async-start | bytes 4866048 | tf_op jit(solution)/shard_map/reduce_scatter | solution.py:377
  1288.1 268.9 %reduce-scatter.12.cloned.1.call-start = ((), (), s32[]{:S(2)}) async-start(), calls=%async_computation.20 | async-start | bytes 4866048 | tf_op jit(solution)/shard_map/reduce_scatter | solution.py:378
  1291.3 514.6 %reduce-scatter.16.cloned.1.call-start = ((), (), s32[]{:S(2)}) async-start(), calls=%async_computation.22 | async-start | bytes 25952256 | tf_op jit(solution)/shard_map/reduce_scatter | solution.py:299
  1301.6 753.8 %reduce-scatter.18.cloned.1.call-start = ((), (), s32[]{:S(2)}) async-start(), calls=%async_computation.23 | async-start | bytes 25952256 | tf_op jit(solution)/shard_map/reduce_scatter | solution.py:300
  1313.1 991.8 %reduce-scatter.20.cloned.1.call-start = ((), (), s32[]{:S(2)}) async-start(), calls=%async_computation.24 | async-start | bytes 25952256 | tf_op jit(solution)/shard_map/reduce_scatter | solution.py:301
  1329.8 7.3 copy-start.10
  1329.8 8.2 copy-start.21
  1337.2 42.5 %copy-start.8 = (f32[128,1536]{1,0:T(8,128)S(1)}, f32[128,1536]{1,0:T(8,128)}, u32[]{:S(2)}) copy-start(f32[128,1536]{1,0:T(8,128)} %copy-done.7) | copy-start | bytes 2359300
  (49 other events, 175.5 us)
Sparse Core Ops, SparseCore 0:
  9.6 38.7 all-gather.11
  49.9 36.0 all-gather.15
  87.5 62.6 all-gather.19
  153.5 69.2 all-gather.13
  225.5 77.1 all-gather.17
  304.2 60.7 all-gather.21
  366.5 152.4 all-gather.23
  520.6 152.4 all-gather.25
  674.7 152.4 all-gather.27
  830.5 119.0 all-gather.29
  953.2 96.7 all-gather.31
  1056.2 134.1 reduce-scatter.7
  1197.0 135.3 reduce-scatter.13
  1338.3 106.4 reduce-scatter.9
  1450.6 106.3 reduce-scatter.11
  1563.9 242.0 reduce-scatter.15
  1812.8 242.5 reduce-scatter.17
  2062.3 242.5 reduce-scatter.19
where the time goes:
time: 2320 us; the launch traced here: 2310 us
  waiting for transfers between devices  1590 us (69%)
  matrix products  346 us (15%)
  blocking collectives  184 us (8%)
  local copies, waits for them, and re-layouts  125 us (5%)
  other arithmetic  39.2 us (2%)
    reduce_scatter x1, waiting for transfers between devices, body(): lax.psum_scatter(local_up, ('ctx', 'shard'), scatter_dimension=0, tiled=T...  249 us
    reduce_scatter x1, waiting for transfers between devices, body(): lax.psum_scatter(local_down, ('ctx', 'shard'), scatter_dimension=0, tiled...  249 us
    reduce_scatter x1, waiting for transfers between devices, body(): lax.psum_scatter(local_gate, ('ctx', 'shard'), scatter_dimension=0, tiled...  249 us
    all_gather x1, waiting for transfers between devices, body(): lax.all_gather(w_up, 'shard', axis=0, tiled=True)  146 us
    all_gather x1, waiting for transfers between devices, body(): lax.all_gather(w_down, 'shard', axis=0, tiled=True)  146 us
    all_gather x1, waiting for transfers between devices, body(): lax.all_gather(w_gate, 'shard', axis=0, tiled=True)  124 us
    reduce_scatter x1, waiting for transfers between devices, body(): lax.psum_scatter(local_value, ('ctx', 'shard'), scatter_dimension=0, tile...  112 us
    dot_general x16, matrix products, score_block(): jnp.einsum('tgjd,sgd->gjts', query_part, key_block, preferred_element_typ...  79.5 us
  transfers between devices with their start and end apart: 18, of which 13 were waited for; matrix products, arithmetic and copies ran while one was open for 22% of the time, Pallas kernels for 0%

commit v1 on v0

v1 whole, which is shorter than its diff:
```python
import functools
import math

import jax
import jax.numpy as jnp
from jax import lax
from jax.experimental import pallas as pl
from jax.experimental.pallas import tpu as pltpu
from jax.sharding import PartitionSpec as P

HEAD = 96
GROUP = 2
EPSILON = 1e-05
ROPE_BASE = 100000.0
LOG2E = math.log2(math.e)
F32 = jnp.float32
BF16 = jnp.bfloat16

NN = (((1,), (0,)), ((), ()))
NT = (((1,), (1,)), ((), ()))
TN = (((0,), (0,)), ((), ()))
TT = (((0,), (1,)), ((), ()))


def dot(a, b, dims):
    return lax.dot_general(a, b, dims, preferred_element_type=F32)


def load_queries(q_ref, qs, blk):
    for part in range(2):
        lanes = slice(part * blk, (part + 1) * blk)
        qs[part] = jnp.concatenate([q_ref[0, j, :, lanes] for j in range(GROUP)], axis=1)


def causal_mask(blk):
    key_row = lax.broadcasted_iota(jnp.int32, (blk, GROUP * blk), 0)
    query_row = lax.broadcasted_iota(jnp.int32, (blk, GROUP * blk), 1) % blk
    return key_row <= query_row


def attention_forward(n, blk, unroll, info, q_ref, kv_ref, o_ref, lse_ref, qs, sc, mx, ls, acc):
    own = info[n]
    mine = info[own]
    factor = LOG2E / math.sqrt(HEAD)
    load_queries(q_ref, qs, blk)
    allowed = causal_mask(blk)

    def fold(value):
        return jnp.max(value, axis=0, keepdims=True)

    def product(c, lane, part):
        keys = kv_ref[c, 0, 0, :, pl.ds(lane, blk)]
        return dot(keys, qs[part], TN)

    diag_a = jnp.where(allowed, product(own, 0, 0), -1e30)
    full_b = product(own, 0, 1)
    diag_b = jnp.where(allowed, product(own, blk, 1), -1e30)
    sc[0], sc[1], sc[2] = diag_a, full_b, diag_b
    mx[0] = fold(diag_a)
    mx[1] = jnp.maximum(fold(full_b), fold(diag_b))

    def other(i):
        c = lax.rem(own + i, n)
        part = jnp.where(info[c] < mine, 0, 1)
        return c, part, pl.multiple_of(part * blk, blk)

    def score_step(i, carry):
        c, part, lane = other(i)
        first = product(c, 0, 1)
        second = product(c, lane, part)
        sc[2 * i + 1] = first
        sc[2 * i + 2] = second
        mx[1] = jnp.maximum(mx[1], fold(first))
        mx[part] = jnp.maximum(mx[part], fold(second))
        return carry

    lax.fori_loop(1, n, score_step, 0, unroll=unroll)
    mx[...] = mx[...] * factor

    def weigh(slot, c, lane, part):
        weights = jnp.exp2(sc[slot] * factor - mx[part])
        values = kv_ref[c, 1, 0, :, pl.ds(lane, blk)]
        return jnp.sum(weights, axis=0, keepdims=True), dot(values, weights.astype(BF16), NN)

    ls[0], acc[0] = weigh(0, own, 0, 0)
    sum_one, mix_one = weigh(1, own, 0, 1)
    sum_two, mix_two = weigh(2, own, blk, 1)
    ls[1] = sum_one + sum_two
    acc[1] = mix_one + mix_two

    def mix_step(i, carry):
        c, part, lane = other(i)
        total, mixed = weigh(2 * i + 1, c, 0, 1)
        ls[1] += total
        acc[1] += mixed
        total, mixed = weigh(2 * i + 2, c, lane, part)
        ls[part] += total
        acc[part] += mixed
        return carry

    lax.fori_loop(1, n, mix_step, 0, unroll=unroll)
    for part in range(2):
        lanes = slice(part * blk, (part + 1) * blk)
        mixed = (acc[part] / ls[part]).astype(BF16)
        total = mx[part] + jnp.log2(ls[part])
        for j in range(GROUP):
            o_ref[0, j, :, lanes] = mixed[:, j * blk : (j + 1) * blk]
            lse_ref[0, j : j + 1, lanes] = total[:, j * blk : (j + 1) * blk]


def attention_backward(
    n, blk, unroll, info, q_ref, g_ref, o_ref, lse_ref, kv_ref, dq_ref, dkv_ref, qs, gs, st, acc
):
    own = info[n]
    mine = info[own]
    scale = 1.0 / math.sqrt(HEAD)
    factor = LOG2E * scale
    load_queries(q_ref, qs, blk)
    load_queries(g_ref, gs, blk)
    allowed = causal_mask(blk)
    for part in range(2):
        lanes = slice(part * blk, (part + 1) * blk)
        for j in range(GROUP):
            cols = slice(j * blk, (j + 1) * blk)
            st[part, 0:1, cols] = lse_ref[0, j : j + 1, lanes]
            st[part, 1:2, cols] = jnp.sum(
                g_ref[0, j, :, lanes].astype(F32) * o_ref[0, j, :, lanes].astype(F32),
                axis=0,
                keepdims=True,
            )

    def product(c, lane, part, masked=False):
        keys = kv_ref[c, 0, 0, :, pl.ds(lane, blk)]
        values = kv_ref[c, 1, 0, :, pl.ds(lane, blk)]
        queries = qs[part]
        grads = gs[part]
        weights = jnp.exp2(dot(keys, queries, TN) * factor - st[part, 0:1])
        if masked:
            weights = jnp.where(allowed, weights, 0.0)
        slope = (weights * (dot(values, grads, TN) - st[part, 1:2])).astype(BF16)
        return (
            dot(queries, slope, NT),
            dot(grads, weights.astype(BF16), NT),
            dot(keys, slope, NN),
        )

    key_a, value_a, acc[0] = product(own, 0, 0, True)
    key_b, value_b, query_b = product(own, 0, 1)
    key_c, value_c, query_c = product(own, blk, 1, True)
    acc[1] = query_b + query_c
    dkv_ref[own, 0, 0, :, 0:blk] = ((key_a + key_b) * scale).astype(BF16)
    dkv_ref[own, 1, 0, :, 0:blk] = (value_a + value_b).astype(BF16)
    dkv_ref[own, 0, 0, :, blk : 2 * blk] = (key_c * scale).astype(BF16)
    dkv_ref[own, 1, 0, :, blk : 2 * blk] = value_c.astype(BF16)

    def step(i, carry):
        c = lax.rem(own + i, n)
        part = jnp.where(info[c] < mine, 0, 1)
        lane = pl.multiple_of(part * blk, blk)
        key_one, value_one, query_one = product(c, 0, 1)
        key_two, value_two, query_two = product(c, lane, part)
        acc[1] += query_one
        acc[part] += query_two
        late = part == 1
        dkv_ref[c, 0, 0, :, 0:blk] = (
            (key_one + jnp.where(late, 0.0, key_two)) * scale
        ).astype(BF16)
        dkv_ref[c, 1, 0, :, 0:blk] = (value_one + jnp.where(late, 0.0, value_two)).astype(BF16)
        dkv_ref[c, 0, 0, :, blk : 2 * blk] = (jnp.where(late, key_two, 0.0) * scale).astype(BF16)
        dkv_ref[c, 1, 0, :, blk : 2 * blk] = jnp.where(late, value_two, 0.0).astype(BF16)
        return carry

    lax.fori_loop(1, n, step, 0, unroll=unroll)
    for part in range(2):
        lanes = slice(part * blk, (part + 1) * blk)
        total = acc[part] * scale
        for j in range(GROUP):
            dq_ref[0, j, :, lanes] = total[:, j * blk : (j + 1) * blk]


def unroll_of(n):
    return 3 if (n - 1) % 3 == 0 else 1


def run_forward(info, queries, kv, n, blk):
    heads = kv.shape[2]
    head_spec = pl.BlockSpec((1, GROUP, HEAD, 2 * blk), lambda g, *_: (g, 0, 0, 0))
    kv_spec = pl.BlockSpec((n, 2, 1, HEAD, 2 * blk), lambda g, *_: (0, 0, g, 0, 0))
    stat_spec = pl.BlockSpec((1, GROUP, 2 * blk), lambda g, *_: (g, 0, 0))
    pairs = heads * GROUP * 33 * blk * blk
    return pl.pallas_call(
        functools.partial(attention_forward, n, blk, unroll_of(n)),
        grid_spec=pltpu.PrefetchScalarGridSpec(
            num_scalar_prefetch=1,
            grid=(heads,),
            in_specs=[head_spec, kv_spec],
            out_specs=[head_spec, stat_spec],
            scratch_shapes=[
                pltpu.VMEM((2, HEAD, GROUP * blk), BF16),
                pltpu.VMEM((2 * n + 1, blk, GROUP * blk), F32),
                pltpu.VMEM((2, 1, GROUP * blk), F32),
                pltpu.VMEM((2, 1, GROUP * blk), F32),
                pltpu.VMEM((2, HEAD, GROUP * blk), F32),
            ],
        ),
        out_shape=[
            jax.ShapeDtypeStruct((heads, GROUP, HEAD, 2 * blk), BF16),
            jax.ShapeDtypeStruct((heads, GROUP, 2 * blk), F32),
        ],
        cost_estimate=pl.CostEstimate(
            flops=4 * HEAD * pairs, bytes_accessed=kv.size * 2, transcendentals=pairs
        ),
        name="attend",
    )(info, queries, kv)


def run_backward(info, queries, grads, outputs, stats, kv, n, blk):
    heads = kv.shape[2]
    head_spec = pl.BlockSpec((1, GROUP, HEAD, 2 * blk), lambda g, *_: (g, 0, 0, 0))
    kv_spec = pl.BlockSpec((n, 2, 1, HEAD, 2 * blk), lambda g, *_: (0, 0, g, 0, 0))
    stat_spec = pl.BlockSpec((1, GROUP, 2 * blk), lambda g, *_: (g, 0, 0))
    pairs = heads * GROUP * 33 * blk * blk
    return pl.pallas_call(
        functools.partial(attention_backward, n, blk, unroll_of(n)),
        grid_spec=pltpu.PrefetchScalarGridSpec(
            num_scalar_prefetch=1,
            grid=(heads,),
            in_specs=[head_spec, head_spec, head_spec, stat_spec, kv_spec],
            out_specs=[head_spec, kv_spec],
            scratch_shapes=[
                pltpu.VMEM((2, HEAD, GROUP * blk), BF16),
                pltpu.VMEM((2, HEAD, GROUP * blk), BF16),
                pltpu.VMEM((2, 2, GROUP * blk), F32),
                pltpu.VMEM((2, HEAD, GROUP * blk), F32),
            ],
        ),
        out_shape=[
            jax.ShapeDtypeStruct((heads, GROUP, HEAD, 2 * blk), F32),
            jax.ShapeDtypeStruct(kv.shape, BF16),
        ],
        cost_estimate=pl.CostEstimate(
            flops=10 * HEAD * pairs, bytes_accessed=kv.size * 4, transcendentals=pairs
        ),
        name="attend_back",
    )(info, queries, grads, outputs, stats, kv)


def rotate(value, cosine, sine):
    half = HEAD // 2
    first, second = value[:, :half], value[:, half:]
    return jnp.concatenate(
        [first * cosine - second * sine, second * cosine + first * sine], axis=1
    )


def rms(value):
    return lax.rsqrt(jnp.mean(value * value, axis=-1, keepdims=True) + EPSILON)


def rms_backward(grad, normed, inverse, gain):
    scaled = grad * gain
    inner = jnp.mean(scaled * normed, axis=-1, keepdims=True)
    return inverse * (scaled - normed * inner)


def body(
    n,
    layer_input,
    positions,
    norm_gain_attn,
    w_query,
    key_weight,
    value_weight,
    w_out,
    norm_gain_ffn,
    w_gate,
    w_up,
    w_down,
    out_cotangent,
):
    c = lax.axis_index("ctx")
    s = lax.axis_index("shard")
    o = 1 - s
    core = lax.rem(c, 2)
    rows, width = layer_input.shape
    half = rows // 2
    blk = 2 * half
    pair_rows = 2 * rows

    def swap(value):
        return lax.ppermute(value, "shard", [(0, 1), (1, 0)])

    def core_swap(value):
        return lax.ppermute(value, "ctx", [(i, i ^ 1) for i in range(n)])

    def columns(weight, index):
        size = weight.shape[1] // 2
        return lax.dynamic_slice_in_dim(weight, index * size, size, 1)

    def gather_columns(*weights):
        k = weights[0].shape[0]
        q = k // 2
        own = jnp.concatenate([columns(w, s) for w in weights], axis=1)
        send = jnp.concatenate(
            [columns(lax.dynamic_slice_in_dim(w, core * q, q, 0), o) for w in weights], axis=1
        )
        near = swap(send)
        far = core_swap(near)
        whole = jnp.zeros((2 * k, own.shape[1]), own.dtype)
        whole = lax.dynamic_update_slice_in_dim(whole, own, s * k, 0)
        whole = lax.dynamic_update_slice_in_dim(whole, near, o * k + core * q, 0)
        return lax.dynamic_update_slice_in_dim(whole, far, o * k + (1 - core) * q, 0)

    def join(own, other):
        own = own.reshape(2, 1, half, -1)
        other = other.reshape(2, 1, half, -1)
        first = jnp.where(s == 0, own, other)
        second = jnp.where(s == 0, other, own)
        return jnp.concatenate([first, second], axis=1).reshape(pair_rows, -1)

    def mine(value):
        value = value.reshape(2, 2, half, -1)
        return lax.dynamic_index_in_dim(value, s, 1, False).reshape(rows, -1)

    def theirs(value):
        value = value.reshape(2, 2, half, -1)
        return lax.dynamic_index_in_dim(value, o, 1, False).reshape(rows, -1)

    resid_in = join(layer_input, swap(layer_input)).astype(F32)
    w_qkv = gather_columns(w_query, key_weight, value_weight)
    cotangent = join(out_cotangent, swap(out_cotangent))
    wg = gather_columns(w_gate)
    wu = gather_columns(w_up)

    numbers = positions.reshape(n, pair_rows)[:, 0] // blk
    info = jnp.concatenate([numbers, c[None]]).astype(jnp.int32)
    pair_positions = lax.dynamic_index_in_dim(
        positions.reshape(n, 2, 2, half), c, 0, False
    ).transpose(1, 0, 2).reshape(pair_rows)
    frequency = ROPE_BASE ** (-2.0 * jnp.arange(HEAD // 2, dtype=F32) / HEAD)
    angles = frequency[:, None] * pair_positions.astype(F32)[None, :]
    cosine, sine = jnp.cos(angles), jnp.sin(angles)

    inverse_one = rms(resid_in)
    normed_one = resid_in * inverse_one
    attn_in = (normed_one * norm_gain_attn).astype(BF16)
    q_half = w_query.shape[1] // 2
    kv_half = key_weight.shape[1] // 2
    heads = kv_half // HEAD
    qkv = dot(w_qkv, attn_in, TT)
    queries = rotate(qkv[:q_half].reshape(-1, HEAD, pair_rows), cosine, sine)
    keys = rotate(qkv[q_half : q_half + kv_half].reshape(-1, HEAD, pair_rows), cosine, sine)
    values = qkv[q_half + kv_half :].reshape(-1, HEAD, pair_rows)
    queries = queries.astype(BF16).reshape(heads, GROUP, HEAD, pair_rows)
    kv_own = jnp.stack([keys, values]).astype(BF16)
    kv = lax.all_gather(kv_own.reshape(2 * kv_half, pair_rows), "ctx").reshape(
        n, 2, heads, HEAD, pair_rows
    )
    attention, stats = run_forward(info, queries, kv, n, blk)
    attention_flat = attention.reshape(q_half, pair_rows)

    partial = dot(attention_flat, w_out, TN).astype(BF16)
    resid_mid = resid_in + (partial.astype(F32) + swap(partial).astype(F32))
    inverse_two = rms(resid_mid)
    normed_two = resid_mid * inverse_two
    ffn_in = (normed_two * norm_gain_ffn).astype(BF16)
    gate = dot(ffn_in, wg, NN)
    upward = dot(ffn_in, wu, NN)
    sigmoid = jax.nn.sigmoid(gate)
    swish = gate * sigmoid
    hidden = (swish * upward).astype(BF16)
    down = dot(hidden, w_down, NN)
    layer_output = (
        mine(resid_mid) + mine(down) + swap(theirs(down).astype(BF16)).astype(F32)
    ).astype(BF16)

    grad_hidden = dot(cotangent, w_down, NT)
    grad_gate_act = (grad_hidden * upward * sigmoid * (1.0 + gate * (1.0 - sigmoid))).astype(BF16)
    grad_up_act = (grad_hidden * swish).astype(BF16)
    partial = (dot(grad_gate_act, wg, NT) + dot(grad_up_act, wu, NT)).astype(BF16)
    grad_normed_two = partial.astype(F32) + swap(partial).astype(F32)
    grad_resid_mid = cotangent.astype(F32) + rms_backward(
        grad_normed_two, normed_two, inverse_two, norm_gain_ffn
    )
    gain_ffn = jnp.sum(mine(grad_normed_two * normed_two), axis=0)
    grad_mid_low = grad_resid_mid.astype(BF16)
    grad_attention = dot(w_out, grad_mid_low, NT).astype(BF16)

    def scatter(value):
        value = value.astype(BF16).reshape(n, value.shape[0] // n, -1)
        return lax.psum_scatter(value, "ctx", scatter_dimension=0, tiled=False)

    def spread_columns(value):
        r = value.shape[0] // 2
        own = lax.dynamic_slice_in_dim(value, s * r, r, 0)
        other = swap(lax.dynamic_slice_in_dim(value, o * r, r, 0))
        first = jnp.where(s == 0, own, other)
        second = jnp.where(s == 0, other, own)
        return jnp.concatenate([first, second], axis=1).astype(F32)

    def spread_rows(value):
        moves = [(2 * i + j, n * j + i) for i in range(n) for j in range(2)]
        return lax.ppermute(value, ("ctx", "shard"), moves).astype(F32)

    grad_down = spread_rows(scatter(dot(hidden, cotangent, TN)))
    grad_gate = spread_columns(scatter(dot(ffn_in, grad_gate_act, TN)))
    grad_up = spread_columns(scatter(dot(ffn_in, grad_up_act, TN)))
    grad_out = spread_rows(scatter(dot(attention_flat, grad_mid_low, NN)))

    grad_query_t, grad_kv = run_backward(
        info,
        queries,
        grad_attention.reshape(queries.shape),
        attention,
        stats,
        kv,
        n,
        blk,
    )
    grad_kv = lax.psum_scatter(
        grad_kv.reshape(n, 2 * kv_half, pair_rows), "ctx", scatter_dimension=0, tiled=False
    ).astype(F32)
    grad_queries = rotate(grad_query_t.reshape(-1, HEAD, pair_rows), cosine, -sine)
    grad_keys = rotate(grad_kv[:kv_half].reshape(-1, HEAD, pair_rows), cosine, -sine)
    grad_qkv = jnp.concatenate(
        [
            grad_queries.reshape(q_half, pair_rows),
            grad_keys.reshape(kv_half, pair_rows),
            grad_kv[kv_half:],
        ]
    ).astype(BF16)
    partial = dot(grad_qkv, w_qkv, TT)
    grad_normed_one = mine(partial) + swap(theirs(partial).astype(BF16)).astype(F32)
    normed_own = mine(normed_one)
    grad_resid_in = rms_backward(grad_normed_one, normed_own, mine(inverse_one), norm_gain_attn)
    gain_attn = jnp.sum(grad_normed_one * normed_own, axis=0)
    input_grad = (mine(grad_resid_mid) + grad_resid_in).astype(BF16)

    local = scatter(dot(attn_in, grad_qkv, TT))
    grad_query = spread_columns(local[:, :q_half])
    grad_key = spread_columns(local[:, q_half : q_half + kv_half])
    grad_value = spread_columns(local[:, q_half + kv_half :])

    gains = jnp.stack([gain_attn.reshape(2 * n, -1), gain_ffn.reshape(2 * n, -1)], axis=1)
    gains = lax.psum_scatter(gains, ("ctx", "shard"), scatter_dimension=0, tiled=False)
    return (
        layer_output,
        input_grad,
        gains[0],
        grad_query,
        grad_key,
        grad_value,
        grad_out,
        gains[1],
        grad_gate,
        grad_up,
        grad_down,
    )


def solution(mesh):
    both = P(("ctx", "shard"), None)
    shard = P("shard", None)
    vector = P(("ctx", "shard"))
    return jax.shard_map(
        functools.partial(body, mesh.shape["ctx"]),
        mesh=mesh,
        in_specs=(both, P(), P(), shard, shard, shard, shard, P(), shard, shard, shard, both),
        out_specs=(both, both, vector, both, both, both, both, vector, both, both, both),
        check_vma=False,
    )
```

time: 2320 us -> 788 us (0.34)
  waiting for transfers between devices: 1590 us -> 488 us
  matrix products: 346 us -> 57.7 us
  blocking collectives: 184 us -> 47.9 us
  local copies, waits for them, and re-layouts: 125 us -> 59.9 us
  Pallas kernels: 0 us -> 54.5 us
  starting transfers between devices: 1.25 us -> 25.4 us
    all_gather x11 -> x1, waiting for transfers between devices: 667 us -> 0.01 us  [body(): lax.all_gather(kv_own.reshape(2 * kv_half, pair_rows), 'ctx')]
    reduce_scatter x7 -> x6, waiting for transfers between devices: 923 us -> 362 us  [the longest x5 303 us: scatter(): return lax.psum_scatter(value, 'ctx', scatter_dimension=0, tiled=False)]
    dot_general x61 -> x15, matrix products: 346 us -> 57.7 us  [dot(): return lax.dot_general(a, b, dims, preferred_element_type=F32)]
    all_gather x2 -> x0, blocking collectives: 147 us -> none  [the longest x1 74.8 us: body(): lax.all_gather(log_rows, ('ctx', 'shard'), axis=0, tiled=True)]
    ppermute x0 -> x19, waiting for transfers between devices: none -> 126 us  [the longest x14 126 us: swap(): return lax.ppermute(value, 'shard', [(0, 1), (1, 0)])]
    pallas_call x0 -> x2, Pallas kernels: none -> 54.5 us  [the longest x1 37 us: run_backward(): pl.pallas_call(functools.partial(attention_backward, n, blk, unroll_of(n)...]
    reshape x19 -> x2, local copies, waits for them, and re-layouts: 36.4 us -> 0.7 us  [the longest x1 0.7 us: body(): positions.reshape(n, 2, 2, half)]
    dynamic_slice x52 -> x14, local copies, waits for them, and re-layouts: 41.9 us -> 16.3 us  [the longest x7 12.3 us: columns(): return lax.dynamic_slice_in_dim(weight, index * size, size, 1)]
  transfers between devices with their start and end apart: 18 -> 26, of which waited for: 13 -> 18; matrix products, arithmetic and copies ran while one was open for 22% -> 14% of each run, Pallas kernels for 0% -> 2%
where the time goes in v1:
time: 788 us; the launch traced here: 779 us
  waiting for transfers between devices  488 us (62%)
  local copies, waits for them, and re-layouts  59.9 us (8%)
  matrix products  57.7 us (7%)
  Pallas kernels  54.5 us (7%)
  blocking collectives  47.9 us (6%)
  other arithmetic  30.4 us (4%)
  starting transfers between devices  25.4 us (3%)
  between operations  15.3 us (2%)
    reduce_scatter x5, waiting for transfers between devices, scatter(): return lax.psum_scatter(value, 'ctx', scatter_dimension=0, tiled=False)  303 us
    ppermute x14, waiting for transfers between devices, swap(): return lax.ppermute(value, 'shard', [(0, 1), (1, 0)])  126 us
    reduce_scatter x1, waiting for transfers between devices, body(): lax.psum_scatter(grad_kv.reshape(n, 2 * kv_half, pair_rows), 'ctx', scatt...  59.3 us
    dot_general x15, matrix products, dot(): return lax.dot_general(a, b, dims, preferred_element_type=F32)  57.7 us
    unnamed x1, blocking collectives  47.9 us
    pallas_call x1, Pallas kernels, run_backward(): pl.pallas_call(functools.partial(attention_backward, n, blk, unroll_of(n)...  37 us
    ppermute x14, starting transfers between devices, swap(): return lax.ppermute(value, 'shard', [(0, 1), (1, 0)])  21.7 us
    pallas_call x1, Pallas kernels, run_forward(): pl.pallas_call(functools.partial(attention_forward, n, blk, unroll_of(n))...  17.6 us
  transfers between devices with their start and end apart: 26, of which 18 were waited for; matrix products, arithmetic and copies ran while one was open for 14% of the time, Pallas kernels for 2%

profile of v1, /device:TPU:0, one launch (start us, length us, event | category | flops | bytes accessed | tf_op | source)
XLA Modules:
  0.0 779.3 jit_solution(11374079985535542756)
XLA Ops:
  24.6 16.7 %collective-permute-done.1 = bf16[384,1536]{1,0:T(8,128)(2,1)} collective-permute-done((bf16[384,1536]{1,0:T(8,128)(2,1)S(1)}, bf16[384,1536]{1,0:T(8,128)(2,1)}, u32[]{:S(2)}, u32[]{:S(2)}) %collective-permute-start.1) | collective-permute-done | bytes 1179680 | tf_op jit(solution)/shard_map/ppermute | solution.py:291
  41.3 8.4 %collective-permute-done = bf16[128,1536]{1,0:T(8,128)(2,1)} collective-permute-done((bf16[128,1536]{1,0:T(8,128)(2,1)}, bf16[128,1536]{1,0:T(8,128)(2,1)}, u32[]{:S(2)}, u32[]{:S(2)}) %collective-permute-start) | collective-permute-done | bytes 393248 | tf_op jit(solution)/shard_map/ppermute | solution.py:291
  49.8 7.6 collective-permute-done.9
  65.3 3.8 fusion.26
  71.3 3.4 dynamic_slice.115
  76.5 3.4 dynamic_slice.113
  80.9 3.6 broadcast.196.clone
  84.5 4.1 dynamic-slice_dynamic-update-slice_fusion
  90.6 21.7 %collective-permute-done.6 = bf16[384,2048]{1,0:T(8,128)(2,1)} collective-permute-done((bf16[384,2048]{1,0:T(8,128)(2,1)}, bf16[384,2048]{1,0:T(8,128)(2,1)}, u32[]{:S(2)}, u32[]{:S(2)}) %collective-permute-start.6) | collective-permute-done | bytes 1572896 | tf_op jit(solution)/shard_map/ppermute | solution.py:291
  115.6 28.7 %collective-permute-done.4 = bf16[384,2048]{1,0:T(8,128)(2,1)} collective-permute-done((bf16[384,2048]{1,0:T(8,128)(2,1)}, bf16[384,2048]{1,0:T(8,128)(2,1)}, u32[]{:S(2)}, u32[]{:S(2)}) %collective-permute-start.4) | collective-permute-done | bytes 1572896 | tf_op jit(solution)/shard_map/ppermute | solution.py:291
  148.0 17.6 %attend.1 = (bf16[4,2,96,256]{3,2,1,0:T(8,128)(2,1)}, f32[4,2,256]{2,1,0:T(2,128)}) custom-call(s32[17]{0:T(128)} %pad_add_fusion.info, bf16[4,2,96,256]{3,2,1,0:T(8,128)(2,1)} %pad_maximum_fusion.4.q_ref, bf16[16,2,4,96,256]{4,3,2,1,0:T(8,128)(2,1)} %bitcast.182), custom_call_target="tpu_custom_call" | custom-call | flops 1660944384 | bytes 6291456 | tf_op jit(solution)/shard_map/attend/pallas_call | solution.py:191
  177.1 10.1 %collective-permute-done.3 = bf16[256,1536]{1,0:T(8,128)(2,1)S(1)} collective-permute-done((bf16[256,1536]{1,0:T(8,128)(2,1)S(1)}, bf16[256,1536]{1,0:T(8,128)(2,1)S(1)}, u32[]{:S(2)}, u32[]{:S(2)}) %collective-permute-start.3) | collective-permute-done | bytes 786464 | tf_op jit(solution)/shard_map/ppermute | solution.py:291
  188.1 5.5 fusion.27
  193.9 3.7 multiply_convert_fusion.1
  197.7 5.4 fusion.30
  206.5 17.6 %collective-permute-done.10 = bf16[256,1536]{1,0:T(8,128)(2,1)S(1)} collective-permute-done((bf16[256,1536]{1,0:T(8,128)(2,1)S(1)}, bf16[256,1536]{1,0:T(8,128)(2,1)S(1)}, u32[]{:S(2)}, u32[]{:S(2)}) %collective-permute-start.10) | collective-permute-done | bytes 786464 | tf_op jit(solution)/shard_map/ppermute | solution.py:291
  229.2 37.0 %attend_back.1 = (f32[4,2,96,256]{3,2,1,0:T(8,128)}, bf16[16,2,4,96,256]{4,3,2,1,0:T(8,128)(2,1)}) custom-call(s32[17]{0:T(128)} %pad_add_fusion.info, bf16[4,2,96,256]{3,2,1,0:T(8,128)(2,1)} %pad_maximum_fusion.4.q_ref, bf16[4,2,96,256]{3,2,1,0:T(8,128)(2,1)} %bitcast.176, bf16[4,2,96,256]{3,2,1,0:T(8,128)(2,1)} %get-tuple-element.15.o_ref, ...), custom_call_target="tpu_custom_call" | custom-call | flops 4152360960 | bytes 12582912 | tf_op jit(solution)/shard_map/attend_back/pallas_call | solution.py:223
  271.0 5.7 convolution_convert_fusion.1
  276.8 5.9 convolution_convert_fusion.2
  283.8 5.7 convolution_convert_fusion
  293.2 59.3 %reduce-scatter.7.cloned.1.call-done = bf16[1,768,256]{2,1,0:T(8,128)(2,1)} async-done(((bf16[16,768,256]{2,1,0:T(8,128)(2,1)}), bf16[1,768,256]{2,1,0:T(8,128)(2,1)}) %reduce-scatter.7.cloned.1.call-update) | async-done | bytes 393232 | tf_op jit(solution)/shard_map/reduce_scatter | solution.py:420
  353.7 3.6 convolution_convert_fusion.3
  358.5 4.8 fusion.28
  368.1 6.5 collective-permute-done.8
  377.2 41.4 %reduce-scatter.11.cloned.1.call-done = bf16[1,48,1536]{2,1,0:T(8,128)(2,1)} async-done(((bf16[16,48,1536]{2,1,0:T(8,128)(2,1)}), bf16[1,48,1536]{2,1,0:T(8,128)(2,1)}) %reduce-scatter.11.cloned.1.call-update) | async-done | bytes 147472 | tf_op jit(solution)/shard_map/reduce_scatter | solution.py:391
  422.0 84.6 %reduce-scatter.15.cloned.1.call-done = bf16[1,96,2048]{2,1,0:T(8,128)(2,1)} async-done(((bf16[16,96,2048]{2,1,0:T(8,128)(2,1)}), bf16[1,96,2048]{2,1,0:T(8,128)(2,1)}) %reduce-scatter.15.cloned.1.call-update) | async-done | bytes 393232 | tf_op jit(solution)/shard_map/reduce_scatter | solution.py:391
  509.0 85.5 %reduce-scatter.13.cloned.1.call-done = bf16[1,96,2048]{2,1,0:T(8,128)(2,1)} async-done(((bf16[16,96,2048]{2,1,0:T(8,128)(2,1)}), bf16[1,96,2048]{2,1,0:T(8,128)(2,1)}) %reduce-scatter.13.cloned.1.call-update) | async-done | bytes 393232 | tf_op jit(solution)/shard_map/reduce_scatter | solution.py:391
  597.0 85.5 %reduce-scatter.17.cloned.1.call-done = bf16[1,128,1536]{2,1,0:T(8,128)(2,1)} async-done(((bf16[16,128,1536]{2,1,0:T(8,128)(2,1)}), bf16[1,128,1536]{2,1,0:T(8,128)(2,1)}) %reduce-scatter.17.cloned.1.call-update) | async-done | bytes 393232 | tf_op jit(solution)/shard_map/reduce_scatter | solution.py:391
  687.4 3.8 fusion.16
  697.5 6.8 collective-permute-done.11
  706.0 47.9 %all-reduce = f32[32,2,48]{2,1,0:T(2,128)S(1)} all-reduce(f32[32,2,48]{2,1,0:T(2,128)S(1)} %pad_maximum_fusion.10), channel_id=3, replica_groups=mesh['ctx'=16,'shard'=2] {'ctx','shard'}, use_global_device_ids=true, to_apply=%region_7.8.clone | all-reduce | flops 3072 | bytes 24576
  757.0 5.9 reduce-scatter.9.cloned.1.call-done
  (247 shorter events, 113.0 us)
Async XLA Ops:
  7.2 158.4 %copy-start = (bf16[768,1536]{1,0:T(8,128)(2,1)S(1)}, bf16[768,1536]{1,0:T(8,128)(2,1)}, u32[]{:S(2)}) copy-start(bf16[768,1536]{1,0:T(8,128)(2,1)} %param.18) | copy-start | bytes 7077892
  7.2 140.8 %all-gather.2.cloned.1.call-start = ((), (), s32[]{:S(2)}) async-start(), calls=%async_computation.6 | async-start | bytes 6684672 | tf_op jit(solution)/shard_map/all_gather | solution.py:356
  11.2 30.1 %collective-permute-start.1 = (bf16[384,1536]{1,0:T(8,128)(2,1)S(1)}, bf16[384,1536]{1,0:T(8,128)(2,1)}, u32[]{:S(2)}, u32[]{:S(2)}) collective-permute-start(bf16[384,1536]{1,0:T(8,128)(2,1)S(1)} %pad_maximum_fusion), channel_id=1, source_target_pairs={{0,1},{1,0},{2,3},{3,2},{4,5},{5,4},{6,7},{7,6},{8,9},{9,8},{10,11... | collective-permute-start | bytes 3538952 | tf_op jit(solution)/shard_map/ppermute | solution.py:291
  14.4 35.4 %collective-permute-start = (bf16[128,1536]{1,0:T(8,128)(2,1)}, bf16[128,1536]{1,0:T(8,128)(2,1)}, u32[]{:S(2)}, u32[]{:S(2)}) collective-permute-start(bf16[128,1536]{1,0:T(8,128)(2,1)} %param.12), channel_id=1, source_target_pairs={{0,1},{1,0},{2,3},{3,2},{4,5},{5,4},{6,7},{7,6},{8,9},{9,8},{10,11... | collective-permute-start | bytes 1179656 | tf_op jit(solution)/shard_map/ppermute | solution.py:291
  14.5 42.8 %collective-permute-start.9 = (bf16[128,1536]{1,0:T(8,128)(2,1)}, bf16[128,1536]{1,0:T(8,128)(2,1)}, u32[]{:S(2)}, u32[]{:S(2)}) collective-permute-start(bf16[128,1536]{1,0:T(8,128)(2,1)} %param.23), channel_id=1, source_target_pairs={{0,1},{1,0},{2,3},{3,2},{4,5},{5,4},{6,7},{7,6},{8,9},{9,8},{10,11... | collective-permute-start | bytes 1179656 | tf_op jit(solution)/shard_map/ppermute | solution.py:291
  41.3 21.6 %collective-permute-start.2 = (bf16[384,1536]{1,0:T(8,128)(2,1)}, bf16[384,1536]{1,0:T(8,128)(2,1)}, u32[]{:S(2)}, u32[]{:S(2)}) collective-permute-start(bf16[384,1536]{1,0:T(8,128)(2,1)} %collective-permute-done.1), channel_id=1, source_target_pairs={{0,2},{2,0},{4,6},{6,4},{8,10},{10,8},{12,14},{14,12},{16,18},{18,... | collective-permute-start | bytes 3538952 | tf_op jit(solution)/shard_map/ppermute | solution.py:294
  59.7 127.6 %copy-start.8 = (bf16[128,1536]{1,0:T(8,128)(2,1)}, bf16[128,1536]{1,0:T(8,128)(2,1)S(1)}, u32[]{:S(2)}) copy-start(bf16[128,1536]{1,0:T(8,128)(2,1)S(1)} %get-tuple-element.62) | copy-start | bytes 1179652
  71.3 281.2 %reduce-scatter.7.cloned.1.call-start = ((), (), s32[]{:S(2)}) async-start(), calls=%async_computation.7 | async-start | bytes 6684672 | tf_op jit(solution)/shard_map/reduce_scatter | solution.py:420
  74.7 37.6 %collective-permute-start.6 = (bf16[384,2048]{1,0:T(8,128)(2,1)}, bf16[384,2048]{1,0:T(8,128)(2,1)}, u32[]{:S(2)}, u32[]{:S(2)}) collective-permute-start(bf16[384,2048]{1,0:T(8,128)(2,1)} %dynamic_slice.115), channel_id=1, source_target_pairs={{0,1},{1,0},{2,3},{3,2},{4,5},{5,4},{6,7},{7,6},{8,9},{9,8},{10,11... | collective-permute-start | bytes 4718600 | tf_op jit(solution)/shard_map/ppermute | solution.py:291
  79.9 64.4 %collective-permute-start.4 = (bf16[384,2048]{1,0:T(8,128)(2,1)}, bf16[384,2048]{1,0:T(8,128)(2,1)}, u32[]{:S(2)}, u32[]{:S(2)}) collective-permute-start(bf16[384,2048]{1,0:T(8,128)(2,1)} %dynamic_slice.113), channel_id=1, source_target_pairs={{0,1},{1,0},{2,3},{3,2},{4,5},{5,4},{6,7},{7,6},{8,9},{9,8},{10,11... | collective-permute-start | bytes 4718600 | tf_op jit(solution)/shard_map/ppermute | solution.py:291
  89.9 57.1 %copy-start.14 = (bf16[1536,2048]{1,0:T(8,128)(2,1)}, bf16[1536,2048]{1,0:T(8,128)(2,1)S(1)}, u32[]{:S(2)}) copy-start(bf16[1536,2048]{1,0:T(8,128)(2,1)S(1)} %dynamic-slice_dynamic-update-slice_fusion.1) | copy-start | bytes 18874372
  112.3 59.3 %collective-permute-start.7 = (bf16[384,2048]{1,0:T(8,128)(2,1)}, bf16[384,2048]{1,0:T(8,128)(2,1)}, u32[]{:S(2)}, u32[]{:S(2)}) collective-permute-start(bf16[384,2048]{1,0:T(8,128)(2,1)} %collective-permute-done.6), channel_id=1, source_target_pairs={{0,2},{2,0},{4,6},{6,4},{8,10},{10,8},{12,14},{14,12},{16,18},{18,... | collective-permute-start | bytes 4718600 | tf_op jit(solution)/shard_map/ppermute | solution.py:294
  144.3 30.0 %collective-permute-start.5 = (bf16[384,2048]{1,0:T(8,128)(2,1)}, bf16[384,2048]{1,0:T(8,128)(2,1)}, u32[]{:S(2)}, u32[]{:S(2)}) collective-permute-start(bf16[384,2048]{1,0:T(8,128)(2,1)} %collective-permute-done.4), channel_id=1, source_target_pairs={{0,2},{2,0},{4,6},{6,4},{8,10},{10,8},{12,14},{14,12},{16,18},{18,... | collective-permute-start | bytes 4718600 | tf_op jit(solution)/shard_map/ppermute | solution.py:294
  167.3 20.0 %collective-permute-start.3 = (bf16[256,1536]{1,0:T(8,128)(2,1)S(1)}, bf16[256,1536]{1,0:T(8,128)(2,1)S(1)}, u32[]{:S(2)}, u32[]{:S(2)}) collective-permute-start(bf16[256,1536]{1,0:T(8,128)(2,1)S(1)} %convolution_convert_fusion.5), channel_id=1, source_target_pairs={{0,1},{1,0},{2,3},{3,2},{4,5},{5,4},{6,7},{7,6},{8,9},{9,8},{10,11... | collective-permute-start | bytes 2359304 | tf_op jit(solution)/shard_map/ppermute | solution.py:291
  205.0 19.1 %collective-permute-start.10 = (bf16[256,1536]{1,0:T(8,128)(2,1)S(1)}, bf16[256,1536]{1,0:T(8,128)(2,1)S(1)}, u32[]{:S(2)}, u32[]{:S(2)}) collective-permute-start(bf16[256,1536]{1,0:T(8,128)(2,1)S(1)} %fusion), channel_id=1, source_target_pairs={{0,1},{1,0},{2,3},{3,2},{4,5},{5,4},{6,7},{7,6},{8,9},{9,8},{10,11... | collective-permute-start | bytes 2359304 | tf_op jit(solution)/shard_map/ppermute | solution.py:291
  266.2 152.4 %reduce-scatter.11.cloned.1.call-start = ((), (), s32[]{:S(2)}) async-start(), calls=%async_computation.9 | async-start | bytes 2506752 | tf_op jit(solution)/shard_map/reduce_scatter | solution.py:391
  269.9 236.6 %reduce-scatter.15.cloned.1.call-start = ((), (), s32[]{:S(2)}) async-start(), calls=%async_computation.11 | async-start | bytes 6684672 | tf_op jit(solution)/shard_map/reduce_scatter | solution.py:391
  276.7 317.8 %reduce-scatter.13.cloned.1.call-start = ((), (), s32[]{:S(2)}) async-start(), calls=%async_computation.10 | async-start | bytes 6684672 | tf_op jit(solution)/shard_map/reduce_scatter | solution.py:391
  282.7 399.9 %reduce-scatter.17.cloned.1.call-start = ((), (), s32[]{:S(2)}) async-start(), calls=%async_computation.12 | async-start | bytes 6684672 | tf_op jit(solution)/shard_map/reduce_scatter | solution.py:391
  289.6 473.3 %reduce-scatter.9.cloned.1.call-start = ((), (), s32[]{:S(2)}) async-start(), calls=%async_computation.8 | async-start | bytes 5013504 | tf_op jit(solution)/shard_map/reduce_scatter | solution.py:391
  291.9 61.8 %copy-start.16 = (bf16[256,1536]{1,0:T(8,128)(2,1)S(1)}, bf16[256,1536]{1,0:T(8,128)(2,1)}, u32[]{:S(2)}) copy-start(bf16[256,1536]{1,0:T(8,128)(2,1)} %copy-done.15) | copy-start | bytes 2359300
  364.1 10.5 %collective-permute-start.8 = (bf16[128,1536]{1,0:T(8,128)(2,1)}, bf16[128,1536]{1,0:T(8,128)(2,1)}, u32[]{:S(2)}, u32[]{:S(2)}) collective-permute-start(bf16[128,1536]{1,0:T(8,128)(2,1)} %bitcast.20), channel_id=1, source_target_pairs={{0,1},{1,0},{2,3},{3,2},{4,5},{5,4},{6,7},{7,6},{8,9},{9,8},{10,11... | collective-permute-start | bytes 1179656 | tf_op jit(solution)/shard_map/ppermute | solution.py:291
  418.6 2.6 collective-permute-start.15
  421.2 266.1 %copy-start.31 = (bf16[4,96,256]{2,1,0:T(8,128)(2,1)S(1)}, bf16[4,96,256]{2,1,0:T(8,128)(2,1)}, u32[]{:S(2)}) copy-start(bf16[4,96,256]{2,1,0:T(8,128)(2,1)} %copy-done.30) | copy-start | bytes 589828
  421.2 266.1 %copy-start.33 = (bf16[384,256]{1,0:T(8,128)(2,1)S(1)}, bf16[384,256]{1,0:T(8,128)(2,1)}, u32[]{:S(2)}) copy-start(bf16[384,256]{1,0:T(8,128)(2,1)} %copy-done.32) | copy-start | bytes 589828
  507.5 176.9 %collective-permute-start.17 = (bf16[48,2048]{1,0:T(8,128)(2,1)S(1)}, bf16[48,2048]{1,0:T(8,128)(2,1)S(1)}, u32[]{:S(2)}, u32[]{:S(2)}) collective-permute-start(bf16[48,2048]{1,0:T(8,128)(2,1)S(1)} %dynamic-slice_bitcast_fusion), channel_id=1, source_target_pairs={{0,1},{1,0},{2,3},{3,2},{4,5},{5,4},{6,7},{7,6},{8,9},{9,8},{10,11... | collective-permute-start | bytes 589832 | tf_op jit(solution)/shard_map/ppermute | solution.py:291
  595.4 90.0 %collective-permute-start.16 = (bf16[48,2048]{1,0:T(8,128)(2,1)S(1)}, bf16[48,2048]{1,0:T(8,128)(2,1)S(1)}, u32[]{:S(2)}, u32[]{:S(2)}) collective-permute-start(bf16[48,2048]{1,0:T(8,128)(2,1)S(1)} %dynamic-slice_bitcast_fusion.1), channel_id=1, source_target_pairs={{0,1},{1,0},{2,3},{3,2},{4,5},{5,4},{6,7},{7,6},{8,9},{9,8},{10,11... | collective-permute-start | bytes 589832 | tf_op jit(solution)/shard_map/ppermute | solution.py:291
  682.5 13.0 %collective-permute-start.18 = (bf16[128,1536]{1,0:T(8,128)(2,1)}, bf16[128,1536]{1,0:T(8,128)(2,1)S(1)}, u32[]{:S(2)}, u32[]{:S(2)}) collective-permute-start(bf16[128,1536]{1,0:T(8,128)(2,1)} %bitcast.184), channel_id=1, source_target_pairs={{0,0},{1,16},{2,1},{3,17},{4,2},{5,18},{6,3},{7,19},{8,4},{9,20},{... | collective-permute-start | bytes 1179656 | tf_op jit(solution)/shard_map/ppermute | solution.py:403
  691.2 13.1 %collective-permute-start.11 = (bf16[128,1536]{1,0:T(8,128)(2,1)S(1)}, bf16[128,1536]{1,0:T(8,128)(2,1)S(1)}, u32[]{:S(2)}, u32[]{:S(2)}) collective-permute-start(bf16[128,1536]{1,0:T(8,128)(2,1)S(1)} %bitcast.177), channel_id=1, source_target_pairs={{0,1},{1,0},{2,3},{3,2},{4,5},{5,4},{6,7},{7,6},{8,9},{9,8},{10,11... | collective-permute-start | bytes 1179656 | tf_op jit(solution)/shard_map/ppermute | solution.py:291
  764.8 4.0 collective-permute-start.14
  766.1 4.0 collective-permute-start.13
  766.9 4.4 collective-permute-start.12
  (46 other events, 442.7 us)
Sparse Core Ops, SparseCore 0:
  71.4 62.8 all-gather.1
  266.3 86.1 reduce-scatter.6
  356.3 62.3 reduce-scatter.10
  422.4 84.0 reduce-scatter.14
  510.3 84.1 reduce-scatter.12
  598.3 84.1 reduce-scatter.16
  686.4 76.4 reduce-scatter.8
